TPU v7x, 256 devices: a whole 4x4x8 slice. The times are simulated.
256 devices in a mesh: section: 4 (over x), dp: 64 (over y, z, core).
Axes of the slice: x: 4, y: 4, z: 8, core: 2. Of those that a mesh axis runs over, the one named last changes fastest.
Arguments:
- acts: bfloat16 [4, 16384, 2560], P('section', 'dp'), may hold values from -6 to 6
- gates: bfloat16 [4, 16384, 1280], P('section', 'dp'), may hold values from -6 to 6
- w_value: bfloat16 [4, 2560, 1280], P('section', 'dp'), may hold values from -0.125 to 0.125
- w_out: bfloat16 [4, 2560, 1280], P('section', 'dp'), may hold values from -0.125 to 0.125
- residual_error: bfloat16 [4, 163840, 1280], P('section', 'dp'), may hold values from -48 to 48
- grad_top: bfloat16 [16384, 2560], P('dp'), may hold values from -6 to 6
- warm_factor: float32 [4, 4, 1280], P('section'), may hold values from -6 to 6
Outputs:
- grad_in: bfloat16 [4, 16384, 2560], P('section', 'dp')
- basis_out: float32 [4, 4, 2560], P('section')
- right_out: float32 [4, 4, 1280], P('section')
All inputs are finite; a program needn't handle non-finite values.
Results may differ from a plain program's by a relative error of at most 0.009.
Values may be sent and summed in bfloat16 or wider, within the bound.
A program may use at most 128 MiB of HBM per device.

v0:
```python
import functools
import math

import jax
import jax.numpy as jnp
from jax import lax
from jax.sharding import Mesh
from jax.sharding import PartitionSpec as P

MICRO = 4
DP = ("dp_0", "dp_1", "dp_2")


HIGHEST_PRECISION = lax.Precision.HIGHEST


def in_one_piece(arrays, axis, dim, along):
    both = jnp.concatenate(arrays, axis=along)
    whole, at, finished = (lax.all_gather(both, axis, axis=dim, tiled=True), 0, [])
    for a in arrays:
        finished.append(lax.slice_in_dim(whole, at, at + a.shape[along], axis=along))
        at += a.shape[along]
    return tuple(finished)


def shifted(value, axis, by):
    peers = lax.axis_size(axis)
    pairs = [(i, i + by) for i in range(peers) if 0 <= i + by < peers]
    return lax.ppermute(value, axis, pairs)


def one_axis_at_a_time(value, axes):
    return functools.reduce(lax.psum, axes, value)


def from_everyone(value, axis):
    peers = lax.axis_size(axis)
    return lax.all_to_all(
        jnp.broadcast_to(value[None], (peers, *value.shape)), axis, 0, 0, tiled=True
    )


def taken_together(value, axis):
    return from_everyone(value, axis).sum(axis=0)


def orthonormal(vectors):
    result = []
    for column in range(vectors.shape[0]):
        current = vectors[column]
        for previous in result:
            current = current - jnp.mean(current * previous) * previous
        current = current / jnp.sqrt(jnp.mean(current * current) + 1e-06)
        result.append(current)
    return jnp.stack(result)


def local(acts, gates, w_value, w_out, residual_error, grad_top, warm_factor):
    value_full, out_full = in_one_piece((w_value[0], w_out[0]), DP, 0, 1)
    section_count = lax.axis_size("section")
    section_index = lax.axis_index("section")
    inputs = acts[0]
    gate_rows = gates[0]
    row_count = inputs.shape[0]
    model_width = inputs.shape[1]
    block_rows = row_count // MICRO
    value_grads = jnp.zeros((row_count, gate_rows.shape[1]), jnp.bfloat16)
    passed_rows = jnp.zeros((row_count, model_width), jnp.bfloat16)
    incoming = jnp.zeros((block_rows, model_width), jnp.bfloat16)
    turn_count = MICRO + section_count - 1
    for step_index in range(turn_count):
        micro_index = step_index - (section_count - 1 - section_index)
        active = (micro_index >= 0) & (micro_index < MICRO)
        offset = jnp.clip(micro_index, 0, MICRO - 1) * block_rows
        top_rows = lax.dynamic_slice_in_dim(grad_top, offset, block_rows, 0)
        arriving = jnp.where(section_index == section_count - 1, top_rows, incoming)
        gate_block = lax.dynamic_slice_in_dim(gate_rows, offset, block_rows, 0)
        hidden = jnp.dot(arriving, out_full, preferred_element_type=jnp.float32)
        value_grad = (hidden * gate_block.astype(jnp.float32)).astype(jnp.bfloat16)
        back_term = lax.dot_general(
            value_grad, value_full, (((1,), (1,)), ((), ())), preferred_element_type=jnp.float32
        )
        passed = (arriving.astype(jnp.float32) + back_term).astype(jnp.bfloat16)
        value_grads = jnp.where(
            active, lax.dynamic_update_slice_in_dim(value_grads, value_grad, offset, 0), value_grads
        )
        passed_rows = jnp.where(
            active, lax.dynamic_update_slice_in_dim(passed_rows, passed, offset, 0), passed_rows
        )
        if step_index + 1 < turn_count:
            incoming = shifted(passed, "section", -1)
    warm_start = warm_factor[0]
    grads_wide = value_grads.astype(jnp.float32)
    inputs_wide = inputs.astype(jnp.float32)
    error_wide = residual_error[0].astype(jnp.float32)
    projected = jnp.dot(grads_wide, warm_start.T, precision=HIGHEST_PRECISION)
    factor = lax.dot_general(
        projected, inputs_wide, (((0,), (0,)), ((), ())), precision=HIGHEST_PRECISION
    )
    factor = factor + lax.dot_general(
        warm_start, error_wide, (((1,), (1,)), ((), ())), precision=HIGHEST_PRECISION
    )
    factor_total = one_axis_at_a_time(factor, DP)
    basis_rows = orthonormal(factor_total)
    mapped = jnp.dot(inputs_wide, basis_rows.T, precision=HIGHEST_PRECISION)
    second = lax.dot_general(
        mapped, grads_wide, (((0,), (0,)), ((), ())), precision=HIGHEST_PRECISION
    )
    second = second + jnp.dot(basis_rows, error_wide, precision=HIGHEST_PRECISION)
    second = taken_together(second, DP) / math.sqrt(row_count * lax.axis_size(DP) * model_width)
    return (passed_rows[None], basis_rows[None], second[None])


def solution(mesh):
    finer = Mesh(
        mesh.devices.reshape(mesh.shape["section"], 4, 8, 2), ("section", "dp_0", "dp_1", "dp_2")
    )
    return jax.shard_map(
        local,
        mesh=finer,
        in_specs=(
            P("section", DP, None),
            P("section", DP, None),
            P("section", DP, None),
            P("section", DP, None),
            P("section", DP, None),
            P(DP, None),
            P("section", None, None),
        ),
        out_specs=(P("section", DP, None), P("section", None, None), P("section", None, None)),
        check_vma=False,
    )
```

profile of v0, /device:TPU:1, one launch (start us, length us, event | category | flops | bytes accessed | tf_op | source)
XLA Modules:
  0.0 348.6 jit_solution(7194534612812928800)
XLA Ops:
  7.2 1.7 pad_maximum_fusion
  9.0 97.2 %all-gather.2.cloned.1.call-done = bf16[2560,2560]{1,0:T(8,128)(2,1)} async-done(((bf16[40,2560]{1,0:T(8,128)(2,1)}), bf16[2560,2560]{1,0:T(8,128)(2,1)}) %all-gather.2.cloned.1.call-update) | async-done | bytes 13107216 | tf_op jit(solution)/shard_map/all_gather | solution.py:19
  106.2 4.2 %select_dynamic-update-slice_fusion.12 = (bf16[256,1280]{1,0:T(8,128)(2,1)S(1)}, bf16[64,1280]{1,0:T(8,128)(2,1)S(1)}) fusion(bf16[256,1280]{1,0:T(8,128)(2,1)S(1)} %broadcast_in_dim.30, s32[]{:T(128)S(6)} %select_n.216, pred[]{:T(512)S(6)} %and.22, bf16[1,256,1280]{2,1,0:T(8,128)(2,1)} %param.8, bf16[2560,2560]{1,0:T(8,128)(2,1)} %all-gather.2.cloned.1.call-done, ...), kind=kOutput, calls=%fused_computation.74 | convolution fusion | flops 419921920 | bytes 7374848 | tf_op jit(solution)/shard_map/dot_general | solution.py:78
  110.5 5.8 %select_dynamic-update-slice_fusion.5 = (bf16[256,2560]{1,0:T(8,128)(2,1)S(1)}, bf16[64,2560]{1,0:T(8,128)(2,1)}) fusion(bf16[256,2560]{1,0:T(8,128)(2,1)S(1)} %broadcast_in_dim.26, s32[]{:T(128)S(6)} %select_n.216, pred[]{:T(512)S(6)} %and.22, bf16[64,1280]{1,0:T(8,128)(2,1)S(1)} %get-tuple-element.35, ...), kind=kOutput, calls=%fused_computation.65 | convolution fusion | flops 420249600 | bytes 7700486 | tf_op jit(solution)/shard_map/dot_general | solution.py:80
  116.3 1.3 collective-permute-start
  117.6 9.9 %collective-permute-done = bf16[64,2560]{1,0:T(8,128)(2,1)} collective-permute-done((bf16[64,2560]{1,0:T(8,128)(2,1)}, bf16[64,2560]{1,0:T(8,128)(2,1)}, u32[]{:S(2)}, u32[]{:S(2)}) %collective-permute-start) | collective-permute-done | bytes 327712 | tf_op jit(solution)/shard_map/ppermute | solution.py:29
  127.5 4.3 %select_dynamic-update-slice_fusion.11 = (bf16[256,1280]{1,0:T(8,128)(2,1)S(1)}, bf16[64,1280]{1,0:T(8,128)(2,1)S(1)}) fusion(bf16[256,1280]{1,0:T(8,128)(2,1)S(1)} %get-tuple-element.34, s32[]{:T(128)S(6)} %select_n.221, pred[]{:T(512)S(6)} %and.23, bf16[1,256,1280]{2,1,0:T(8,128)(2,1)} %param.8, bf16[2560,2560]{1,0:T(8,128)(2,1)} %all-gather.2.cloned.1.call-done, ...), kind=kOutput, calls=%fused_computation.73 | convolution fusion | flops 419921920 | bytes 7866368 | tf_op jit(solution)/shard_map/dot_general | solution.py:78
  131.9 5.9 %select_dynamic-update-slice_fusion.4 = (bf16[256,2560]{1,0:T(8,128)(2,1)S(1)}, bf16[64,2560]{1,0:T(8,128)(2,1)}) fusion(bf16[256,2560]{1,0:T(8,128)(2,1)S(1)} %get-tuple-element.32, s32[]{:T(128)S(6)} %select_n.221, pred[]{:T(512)S(6)} %and.23, bf16[64,2560]{1,0:T(8,128)(2,1)} %collective-permute-done, bf16[256,2560]{1,0:T(8,128)(2,1)} %param.12, ...), kind=kOutput, calls=%fused_computation.63 | convolution fusion | flops 420249600 | bytes 8355846 | tf_op jit(solution)/shard_map/dot_general | solution.py:80
  137.8 1.3 collective-permute-start.1
  139.1 9.0 %collective-permute-done.1 = bf16[64,2560]{1,0:T(8,128)(2,1)} collective-permute-done((bf16[64,2560]{1,0:T(8,128)(2,1)}, bf16[64,2560]{1,0:T(8,128)(2,1)}, u32[]{:S(2)}, u32[]{:S(2)}) %collective-permute-start.1) | collective-permute-done | bytes 327712 | tf_op jit(solution)/shard_map/ppermute | solution.py:29
  148.1 4.3 %select_dynamic-update-slice_fusion.10 = (bf16[256,1280]{1,0:T(8,128)(2,1)S(1)}, bf16[64,1280]{1,0:T(8,128)(2,1)S(1)}) fusion(bf16[256,1280]{1,0:T(8,128)(2,1)S(1)} %get-tuple-element.36, s32[]{:T(128)S(6)} %select_n.227, pred[]{:T(512)S(6)} %and.24, bf16[1,256,1280]{2,1,0:T(8,128)(2,1)} %param.8, bf16[2560,2560]{1,0:T(8,128)(2,1)} %all-gather.2.cloned.1.call-done, ...), kind=kOutput, calls=%fused_computation.72 | convolution fusion | flops 419921920 | bytes 7866368 | tf_op jit(solution)/shard_map/dot_general | solution.py:78
  152.4 5.9 %select_dynamic-update-slice_fusion.3 = (bf16[256,2560]{1,0:T(8,128)(2,1)S(1)}, bf16[64,2560]{1,0:T(8,128)(2,1)}) fusion(bf16[256,2560]{1,0:T(8,128)(2,1)S(1)} %get-tuple-element.30, s32[]{:T(128)S(6)} %select_n.227, pred[]{:T(512)S(6)} %and.24, bf16[64,2560]{1,0:T(8,128)(2,1)} %collective-permute-done.1, bf16[256,2560]{1,0:T(8,128)(2,1)} %param.12, ...), kind=kOutput, calls=%fused_computation.61 | convolution fusion | flops 420249600 | bytes 8355846 | tf_op jit(solution)/shard_map/dot_general | solution.py:80
  158.3 1.3 collective-permute-start.2
  159.6 8.2 %collective-permute-done.2 = bf16[64,2560]{1,0:T(8,128)(2,1)} collective-permute-done((bf16[64,2560]{1,0:T(8,128)(2,1)}, bf16[64,2560]{1,0:T(8,128)(2,1)}, u32[]{:S(2)}, u32[]{:S(2)}) %collective-permute-start.2) | collective-permute-done | bytes 327712 | tf_op jit(solution)/shard_map/ppermute | solution.py:29
  167.8 4.3 %select_dynamic-update-slice_fusion.9 = (bf16[256,1280]{1,0:T(8,128)(2,1)S(1)}, bf16[64,1280]{1,0:T(8,128)(2,1)S(1)}) fusion(bf16[256,1280]{1,0:T(8,128)(2,1)S(1)} %get-tuple-element.38, s32[]{:T(128)S(6)} %select_n.233, pred[]{:T(512)S(6)} %and.25, bf16[1,256,1280]{2,1,0:T(8,128)(2,1)} %param.8, bf16[2560,2560]{1,0:T(8,128)(2,1)} %all-gather.2.cloned.1.call-done, ...), kind=kOutput, calls=%fused_computation.71 | convolution fusion | flops 419921920 | bytes 7866368 | tf_op jit(solution)/shard_map/dot_general | solution.py:78
  172.2 5.9 %select_dynamic-update-slice_fusion.2 = (bf16[256,2560]{1,0:T(8,128)(2,1)S(1)}, bf16[64,2560]{1,0:T(8,128)(2,1)}) fusion(bf16[256,2560]{1,0:T(8,128)(2,1)S(1)} %get-tuple-element.28, s32[]{:T(128)S(6)} %select_n.233, pred[]{:T(512)S(6)} %and.25, bf16[64,2560]{1,0:T(8,128)(2,1)} %collective-permute-done.2, bf16[256,2560]{1,0:T(8,128)(2,1)} %param.12, ...), kind=kOutput, calls=%fused_computation.59 | convolution fusion | flops 420249600 | bytes 8355846 | tf_op jit(solution)/shard_map/dot_general | solution.py:80
  178.0 1.3 collective-permute-start.3
  179.3 7.3 %collective-permute-done.3 = bf16[64,2560]{1,0:T(8,128)(2,1)} collective-permute-done((bf16[64,2560]{1,0:T(8,128)(2,1)}, bf16[64,2560]{1,0:T(8,128)(2,1)}, u32[]{:S(2)}, u32[]{:S(2)}) %collective-permute-start.3) | collective-permute-done | bytes 327712 | tf_op jit(solution)/shard_map/ppermute | solution.py:29
  186.7 4.3 %select_dynamic-update-slice_fusion.8 = (bf16[256,1280]{1,0:T(8,128)(2,1)S(1)}, bf16[64,1280]{1,0:T(8,128)(2,1)S(1)}) fusion(bf16[256,1280]{1,0:T(8,128)(2,1)S(1)} %get-tuple-element.40, s32[]{:T(128)S(6)} %select_n.239, pred[]{:T(512)S(6)} %and.26, bf16[1,256,1280]{2,1,0:T(8,128)(2,1)} %param.8, bf16[2560,2560]{1,0:T(8,128)(2,1)} %all-gather.2.cloned.1.call-done, ...), kind=kOutput, calls=%fused_computation.70 | convolution fusion | flops 419921920 | bytes 7866368 | tf_op jit(solution)/shard_map/dot_general | solution.py:78
  191.0 5.8 %select_dynamic-update-slice_fusion.1 = (bf16[256,2560]{1,0:T(8,128)(2,1)S(1)}, bf16[64,2560]{1,0:T(8,128)(2,1)}) fusion(bf16[256,2560]{1,0:T(8,128)(2,1)S(1)} %get-tuple-element.26, s32[]{:T(128)S(6)} %select_n.239, pred[]{:T(512)S(6)} %and.26, bf16[64,2560]{1,0:T(8,128)(2,1)} %collective-permute-done.3, bf16[256,2560]{1,0:T(8,128)(2,1)} %param.12, ...), kind=kOutput, calls=%fused_computation.57 | convolution fusion | flops 420249600 | bytes 8355846 | tf_op jit(solution)/shard_map/dot_general | solution.py:80
  196.9 1.3 collective-permute-start.4
  198.2 6.8 %collective-permute-done.4 = bf16[64,2560]{1,0:T(8,128)(2,1)} collective-permute-done((bf16[64,2560]{1,0:T(8,128)(2,1)}, bf16[64,2560]{1,0:T(8,128)(2,1)}, u32[]{:S(2)}, u32[]{:S(2)}) %collective-permute-start.4) | collective-permute-done | bytes 327712 | tf_op jit(solution)/shard_map/ppermute | solution.py:29
  205.0 4.4 %select_dynamic-update-slice_fusion.7 = (bf16[256,1280]{1,0:T(8,128)(2,1)S(1)}, bf16[64,1280]{1,0:T(8,128)(2,1)S(1)}) fusion(bf16[256,1280]{1,0:T(8,128)(2,1)S(1)} %get-tuple-element.42, s32[]{:T(128)S(6)} %select_n.245, pred[]{:T(512)S(6)} %and.27, bf16[1,256,1280]{2,1,0:T(8,128)(2,1)} %param.8, bf16[2560,2560]{1,0:T(8,128)(2,1)} %all-gather.2.cloned.1.call-done, ...), kind=kOutput, calls=%fused_computation.69 | convolution fusion | flops 419921920 | bytes 7866368 | tf_op jit(solution)/shard_map/dot_general | solution.py:78
  209.5 5.1 %select_dynamic-update-slice_fusion = (bf16[256,2560]{1,0:T(8,128)(2,1)S(1)}, bf16[64,2560]{1,0:T(8,128)(2,1)S(1)}) fusion(bf16[256,2560]{1,0:T(8,128)(2,1)S(1)} %get-tuple-element.24, s32[]{:T(128)S(6)} %select_n.245, pred[]{:T(512)S(6)} %and.27, bf16[64,2560]{1,0:T(8,128)(2,1)} %collective-permute-done.4, bf16[256,2560]{1,0:T(8,128)(2,1)S(1)} %copy-done.3, ...), kind=kOutput, calls=%fused_computation.55 | convolution fusion | flops 420249600 | bytes 8355846 | tf_op jit(solution)/shard_map/dot_general | solution.py:80
  214.6 1.5 collective-permute-start.5
  216.1 5.2 %fusion.2 = f32[4,2560]{1,0:T(4,128)S(1)} fusion(bf16[1,2560,1280]{2,1,0:T(8,128)(2,1)S(1)} %bitcast.59, f32[1,4,1280]{2,1,0:T(4,128)S(1)} %copy-done.2), kind=kOutput, calls=%fused_computation.2 | convolution fusion | flops 157286400 | bytes 6615040 | tf_op jit(solution)/shard_map/dot_general | solution.py:100
  221.3 1.1 collective-permute-done.5
  222.4 4.2 %select_dynamic-update-slice_fusion.6 = (bf16[256,1280]{1,0:T(8,128)(2,1)S(1)}, bf16[64,1280]{1,0:T(8,128)(2,1)S(1)}) fusion(bf16[256,1280]{1,0:T(8,128)(2,1)S(1)} %get-tuple-element.44, s32[]{:T(128)S(6)} %select_n.251, pred[]{:T(512)S(6)} %and.28, bf16[1,256,1280]{2,1,0:T(8,128)(2,1)} %param.8, bf16[2560,2560]{1,0:T(8,128)(2,1)} %all-gather.2.cloned.1.call-done, ...), kind=kOutput, calls=%fused_computation.68 | convolution fusion | flops 419921920 | bytes 7866368 | tf_op jit(solution)/shard_map/dot_general | solution.py:78
  227.2 0.7 convolution_add_fusion.1
  227.9 12.1 %psum.21 = f32[4,2560]{1,0:T(4,128)S(1)} all-reduce(f32[4,2560]{1,0:T(4,128)S(1)} %convolution_add_fusion.1), channel_id=1, replica_groups=mesh['section'=4,'dp_0'=4,'dp_1'=8,'dp_2'=2] {'dp_0'}, use_global_device_ids=true, to_apply=%region_0.1 | all-reduce | flops 10240 | bytes 81920 | tf_op jit(solution)/shard_map/psum | solution.py:33
  240.0 22.4 %psum.22 = f32[4,2560]{1,0:T(4,128)S(1)} all-reduce(f32[4,2560]{1,0:T(4,128)S(1)} %psum.21), channel_id=1, replica_groups=mesh['section'=4,'dp_0'=4,'dp_1'=8,'dp_2'=2] {'dp_1'}, use_global_device_ids=true, to_apply=%region_1.2 | all-reduce | flops 10240 | bytes 81920 | tf_op jit(solution)/shard_map/psum | solution.py:33
  262.4 19.4 %psum.23 = f32[4,2560]{1,0:T(4,128)S(1)} all-reduce(f32[4,2560]{1,0:T(4,128)S(1)} %psum.22), channel_id=1, replica_groups=mesh['section'=4,'dp_0'=4,'dp_1'=8,'dp_2'=2] {'dp_2'}, use_global_device_ids=true, to_apply=%region_2.3 | all-reduce | flops 10240 | bytes 81920 | tf_op jit(solution)/shard_map/psum | solution.py:33
  281.7 0.7 slice_reduce_fusion
  283.2 0.6 multiply_reduce_fusion.8
  284.4 0.6 multiply_reduce_fusion.3
  287.0 0.6 multiply_reduce_fusion.2
  288.9 0.6 multiply_reduce_fusion.4
  290.2 0.6 multiply_reduce_fusion.1
  291.5 0.6 multiply_reduce_fusion
  292.9 1.1 fusion.32
  294.0 4.8 %fusion = f32[4,1280]{1,0:T(4,128)S(1)} fusion(bf16[1,2560,1280]{2,1,0:T(8,128)(2,1)} %param.11, f32[1,2560]{1,0:T(1,128)S(1)} %get-tuple-element.12, f32[1,2560]{1,0:T(1,128)S(1)} %get-tuple-element.13, f32[1,2560]{1,0:T(1,128)S(1)} %get-tuple-element.14, f32[1,2560]{1,0:T(1,128)S(1)} %get-tuple-element.21), kind=kOutput, calls=%fused_computation | convolution fusion | flops 157317120 | bytes 6615040 | tf_op jit(solution)/shard_map/dot_general | solution.py:109
  299.1 1.2 broadcast_in_dim.33
  300.4 6.4 %all-to-all-start = ((f32[64,4,1280]{2,1,0:T(4,128)}), f32[64,4,1280]{2,1,0:T(4,128)S(1)}, u32[]{:S(2)}, u32[]{:S(2)}) async-start(f32[64,4,1280]{2,1,0:T(4,128)} %broadcast_in_dim.33), calls=%async_computation | async-start | bytes 2621440 | tf_op jit(solution)/shard_map/all_to_all | solution.py:38
  306.7 2.5 copy.25
  309.2 0.7 fusion.50
  309.9 6.0 %fusion.37 = bf16[1,256,2560]{2,1,0:T(8,128)(2,1)} fusion(bf16[1,256,2560]{2,1,0:T(8,128)(2,1)} %copy.25, s32[]{:T(128)S(6)} %select_n.251, bf16[256,2560]{1,0:T(8,128)(2,1)} %copy-done.1, pred[]{:T(512)S(6)} %and.28, bf16[64,2560]{1,0:T(8,128)(2,1)} %copy-done.4, bf16[256,2560]{1,0:T(8,128)(2,1)} %param.12, pred[]{:T(512)S(6)} %eq.2, ...), kind=kOutput, calls=%fused_computation.53 | convolution fusion | flops 420249600 | bytes 8028166 | tf_op jit(solution)/shard_map/dot_general | solution.py:80
  315.9 25.0 %all-to-all-done = f32[64,4,1280]{2,1,0:T(4,128)S(1)} async-done(((f32[64,4,1280]{2,1,0:T(4,128)}), f32[64,4,1280]{2,1,0:T(4,128)S(1)}, u32[]{:S(2)}, u32[]{:S(2)}) %all-to-all-start) | async-done | bytes 1310752 | tf_op jit(solution)/shard_map/all_to_all | solution.py:38
  341.1 0.6 multiply_bitcast_fusion
  (24 shorter events, 1.5 us)
Async XLA Ops:
  7.2 220.1 %copy-start = (bf16[1,256,2560]{2,1,0:T(8,128)(2,1)S(1)}, bf16[1,256,2560]{2,1,0:T(8,128)(2,1)}, u32[]{:S(2)}) copy-start(bf16[1,256,2560]{2,1,0:T(8,128)(2,1)} %param.7) | copy-start | bytes 3932164
  7.2 99.0 %all-gather.2.cloned.1.call-start = ((), (), s32[]{:S(2)}) async-start(), calls=%async_computation.1 | async-start | bytes 13312000 | tf_op jit(solution)/shard_map/all_gather | solution.py:19
  116.3 11.2 %collective-permute-start = (bf16[64,2560]{1,0:T(8,128)(2,1)}, bf16[64,2560]{1,0:T(8,128)(2,1)}, u32[]{:S(2)}, u32[]{:S(2)}) collective-permute-start(bf16[64,2560]{1,0:T(8,128)(2,1)} %get-tuple-element.33), channel_id=1, source_target_pairs={{64,0},{128,64},{192,128},{65,1},{129,65},{193,129},{66,2},{130,66... | collective-permute-start | bytes 983048 | tf_op jit(solution)/shard_map/ppermute | solution.py:29
  137.8 10.3 %collective-permute-start.1 = (bf16[64,2560]{1,0:T(8,128)(2,1)}, bf16[64,2560]{1,0:T(8,128)(2,1)}, u32[]{:S(2)}, u32[]{:S(2)}) collective-permute-start(bf16[64,2560]{1,0:T(8,128)(2,1)} %get-tuple-element.31), channel_id=1, source_target_pairs={{64,0},{128,64},{192,128},{65,1},{129,65},{193,129},{66,2},{130,66... | collective-permute-start | bytes 983048 | tf_op jit(solution)/shard_map/ppermute | solution.py:29
  158.3 9.5 %collective-permute-start.2 = (bf16[64,2560]{1,0:T(8,128)(2,1)}, bf16[64,2560]{1,0:T(8,128)(2,1)}, u32[]{:S(2)}, u32[]{:S(2)}) collective-permute-start(bf16[64,2560]{1,0:T(8,128)(2,1)} %get-tuple-element.29), channel_id=1, source_target_pairs={{64,0},{128,64},{192,128},{65,1},{129,65},{193,129},{66,2},{130,66... | collective-permute-start | bytes 983048 | tf_op jit(solution)/shard_map/ppermute | solution.py:29
  178.0 8.6 %collective-permute-start.3 = (bf16[64,2560]{1,0:T(8,128)(2,1)}, bf16[64,2560]{1,0:T(8,128)(2,1)}, u32[]{:S(2)}, u32[]{:S(2)}) collective-permute-start(bf16[64,2560]{1,0:T(8,128)(2,1)} %get-tuple-element.27), channel_id=1, source_target_pairs={{64,0},{128,64},{192,128},{65,1},{129,65},{193,129},{66,2},{130,66... | collective-permute-start | bytes 983048 | tf_op jit(solution)/shard_map/ppermute | solution.py:29
  196.9 8.1 %collective-permute-start.4 = (bf16[64,2560]{1,0:T(8,128)(2,1)}, bf16[64,2560]{1,0:T(8,128)(2,1)}, u32[]{:S(2)}, u32[]{:S(2)}) collective-permute-start(bf16[64,2560]{1,0:T(8,128)(2,1)} %get-tuple-element.25), channel_id=1, source_target_pairs={{64,0},{128,64},{192,128},{65,1},{129,65},{193,129},{66,2},{130,66... | collective-permute-start | bytes 983048 | tf_op jit(solution)/shard_map/ppermute | solution.py:29
  198.2 11.3 %copy-start.3 = (bf16[256,2560]{1,0:T(8,128)(2,1)S(1)}, bf16[256,2560]{1,0:T(8,128)(2,1)}, u32[]{:S(2)}) copy-start(bf16[256,2560]{1,0:T(8,128)(2,1)} %param.12) | copy-start | bytes 3932164
  205.0 11.1 %slice-start = ((s8[6553600]{0:T(1024)(128)(4,1)}), s8[4194304]{0:T(1024)(128)(4,1)S(1)}, s32[]{:S(2)}) async-start(s8[6553600]{0:T(1024)(128)(4,1)} %bitcast.58), calls=%async_computation.2 | async-start | bytes 8388608
  209.4 6.6 %copy-start.2 = (f32[1,4,1280]{2,1,0:T(4,128)S(1)}, f32[1,4,1280]{2,1,0:T(4,128)}, u32[]{:S(2)}) copy-start(f32[1,4,1280]{2,1,0:T(4,128)} %param.13) | copy-start | bytes 61444
  209.5 6.6 %slice-start.1 = ((s8[6553600]{0:T(1024)(128)(4,1)}), s8[2359296]{0:T(1024)(128)(4,1)S(1)}, s32[]{:S(2)}) async-start(s8[6553600]{0:T(1024)(128)(4,1)} %bitcast.58), calls=%async_computation.3 | async-start | bytes 4718592
  214.6 12.1 %copy-start.1 = (bf16[256,2560]{1,0:T(8,128)(2,1)}, bf16[256,2560]{1,0:T(8,128)(2,1)S(1)}, u32[]{:S(2)}) copy-start(bf16[256,2560]{1,0:T(8,128)(2,1)S(1)} %get-tuple-element.22) | copy-start | bytes 3932164
  214.6 7.8 %collective-permute-start.5 = (bf16[64,2560]{1,0:T(8,128)(2,1)S(1)}, bf16[64,2560]{1,0:T(8,128)(2,1)S(1)}, u32[]{:S(2)}, u32[]{:S(2)}) collective-permute-start(bf16[64,2560]{1,0:T(8,128)(2,1)S(1)} %get-tuple-element.23), channel_id=1, source_target_pairs={{64,0},{128,64},{192,128},{65,1},{129,65},{193,129},{66,2},{130,66... | collective-permute-start | bytes 983048 | tf_op jit(solution)/shard_map/ppermute | solution.py:29
  222.4 4.2 %copy-start.4 = (bf16[64,2560]{1,0:T(8,128)(2,1)}, bf16[64,2560]{1,0:T(8,128)(2,1)S(1)}, u32[]{:S(2)}) copy-start(bf16[64,2560]{1,0:T(8,128)(2,1)S(1)} %collective-permute-done.5) | copy-start | bytes 983044
  300.4 40.5 %all-to-all-start = ((f32[64,4,1280]{2,1,0:T(4,128)}), f32[64,4,1280]{2,1,0:T(4,128)S(1)}, u32[]{:S(2)}, u32[]{:S(2)}) async-start(f32[64,4,1280]{2,1,0:T(4,128)} %broadcast_in_dim.33), calls=%async_computation | async-start | bytes 2621440 | tf_op jit(solution)/shard_map/all_to_all | solution.py:38
Sparse Core Ops, SparseCore 0:
  11.3 94.7 all-gather.1
where the time goes:
time: 349 us
  waiting for transfers between devices  165 us (47%)
  matrix products  83.3 us (24%)
  blocking collectives  53.8 us (15%)
  between operations  21 us (6%)
  starting transfers between devices  14.3 us (4%)
  other arithmetic  7.68 us (2%)
  local copies, waits for them, and re-layouts  3.87 us (1%)
    all_gather x1, waiting for transfers between devices, in_one_piece(): lax.all_gather(both, axis, axis=dim, tiled=True)  97.2 us
    psum x3, blocking collectives, one_axis_at_a_time(): return functools.reduce(lax.psum, axes, value)  53.8 us
    ppermute x6, waiting for transfers between devices, shifted(): return lax.ppermute(value, axis, pairs)  42.4 us
    dot_general x7, matrix products, local(): lax.dot_general(value_grad, value_full, (((1,), (1,)), ((), ())), preferr...  40.5 us
    dot_general x7, matrix products, local(): hidden = jnp.dot(arriving, out_full, preferred_element_type=jnp.float32)  30.2 us
    all_to_all x1, waiting for transfers between devices, from_everyone(): lax.all_to_all(jnp.broadcast_to(value[None], (peers, *value.shape)), axis...  25 us
    ppermute x6, starting transfers between devices, shifted(): return lax.ppermute(value, axis, pairs)  7.87 us
  transfers between devices with their start and end apart: 8, of which 8 were waited for; matrix products, arithmetic and copies ran while one was open for 4% of the time, Pallas kernels for 0%

commit v1 on v0

--- a/solution.py
+++ b/solution.py
@@ -4,14 +4,168 @@
 import jax
 import jax.numpy as jnp
 from jax import lax
+from jax.experimental import pallas as pl
+from jax.experimental.pallas import tpu as pltpu
 from jax.sharding import Mesh
 from jax.sharding import PartitionSpec as P
 
+MESH = pl.DeviceIdType.MESH
+F32, BF16 = jnp.float32, jnp.bfloat16
+RANK = 4
+GROUP = 8
+NZ = 8
+
+
+def parts_of(v):
+    high = v.astype(BF16)
+    rest = v - high.astype(F32)
+    mid = rest.astype(BF16)
+    low = (rest - mid.astype(F32)).astype(BF16)
+    stack = [high.astype(F32), mid.astype(F32), low.astype(F32), jnp.zeros_like(v)]
+    return jnp.concatenate(stack, axis=0).astype(BF16)
+
+
+def joined(t):
+    return t[0:RANK] + (t[RANK : 2 * RANK] + t[2 * RANK : 3 * RANK])
+
+
+def dot_nn(a, b):
+    return lax.dot_general(a, b, (((1,), (0,)), ((), ())), preferred_element_type=F32)
+
+
+def dot_nt(a, b):
+    return lax.dot_general(a, b, (((1,), (1,)), ((), ())), preferred_element_type=F32)
+
+
+def orthonormal(vectors):
+    result = []
+    width = vectors.shape[1]
+    for j in range(RANK):
+        current = vectors[j : j + 1]
+        for previous in result:
+            current = current - (jnp.sum(current * previous, axis=1, keepdims=True) / width) * previous
+        norm = jnp.sqrt(jnp.sum(current * current, axis=1, keepdims=True) / width + 1e-06)
+        current = current / norm
+        result.append(current)
+    return jnp.concatenate(result, axis=0)
+
+
+def all_reduced(value, width, src, rs, zs, out, send, recv):
+    y, z, core = lax.axis_index("y"), lax.axis_index("z"), lax.axis_index("core")
+    me = y * 2 + core
+    total = value.shape[1]
+    for piece in range(GROUP):
+        lo, hi = piece * width, min((piece + 1) * width, total)
+        if hi > lo:
+            src[piece, :, 0 : hi - lo] = value[:, lo:hi]
+        if hi - lo < width:
+            src[piece, :, max(hi - lo, 0) : width] = jnp.zeros((RANK, width - max(hi - lo, 0)), F32)
+    rs[me] = src[me]
+
+    def to_group(step, from_ref, dst, phase):
+        peer = lax.rem(me + step, GROUP)
+        return pltpu.make_async_remote_copy(
+            src_ref=from_ref(peer), dst_ref=dst.at[me],
+            send_sem=send.at[phase, step], recv_sem=recv.at[phase, step],
+            device_id={"y": peer // 2, "core": lax.rem(peer, 2)}, device_id_type=MESH)
+
+    def to_line(step):
+        peer = lax.rem(z + step, NZ)
+        return pltpu.make_async_remote_copy(
+            src_ref=zs.at[z], dst_ref=zs.at[z],
+            send_sem=send.at[1, step], recv_sem=recv.at[1, step],
+            device_id={"z": peer}, device_id_type=MESH)
+
+    first = [to_group(s, lambda p: src.at[p], rs, 0) for s in range(1, GROUP)]
+    for c in first:
+        c.start()
+    for c in first:
+        c.wait()
+    acc = rs[0]
+    for i in range(1, GROUP):
+        acc = acc + rs[i]
+    zs[z] = acc
+    second = [to_line(s) for s in range(1, NZ)]
+    for c in second:
+        c.start()
+    for c in second:
+        c.wait()
+    acc = zs[0]
+    for i in range(1, NZ):
+        acc = acc + zs[i]
+    out[me] = acc
+    third = [to_group(s, lambda p: out.at[me], out, 2) for s in range(1, GROUP)]
+    for c in third:
+        c.start()
+    for c in third:
+        c.wait()
+    pieces = [out[i] for i in range((total + width - 1) // width)]
+    return jnp.concatenate(pieces, axis=1)[:, :total]
+
+
+def entry_barrier():
+    y, z, core = lax.axis_index("y"), lax.axis_index("z"), lax.axis_index("core")
+    me = y * 2 + core
+    barrier = pltpu.get_barrier_semaphore()
+    for step in range(1, GROUP):
+        peer = lax.rem(me + step, GROUP)
+        pl.semaphore_signal(barrier, inc=1, device_id={"y": peer // 2, "core": lax.rem(peer, 2)}, device_id_type=MESH)
+    for step in range(1, NZ):
+        pl.semaphore_signal(barrier, inc=1, device_id={"z": lax.rem(z + step, NZ)}, device_id_type=MESH)
+    pl.semaphore_wait(barrier, GROUP + NZ - 2)
+
+
+def powersgd_kernel(scale, acts, vg, err, warm, basis_out, right_out,
+                    src1, rs1, zs1, out1, send1, recv1, src2, rs2, zs2, out2, send2, recv2):
+    entry_barrier()
+    w = parts_of(warm[...])
+    projected = joined(dot_nt(w, vg[...]))
+    width = acts.shape[1]
+    step = 512
+    p = parts_of(projected)
+    cols = []
+    for at in range(0, width, step):
+        t = dot_nn(p, acts[:, at : at + step]) + dot_nt(w, err[at : at + step, :])
+        cols.append(joined(t))
+    factor = all_reduced(jnp.concatenate(cols, axis=1), 384, src1, rs1, zs1, out1, send1, recv1)
+    basis = orthonormal(factor)
+    basis_out[...] = basis
+    b = parts_of(basis)
+    m = parts_of(joined(dot_nt(b, acts[...])))
+    t = dot_nn(m, vg[...]) + dot_nn(b, err[...])
+    right = all_reduced(joined(t), 256, src2, rs2, zs2, out2, send2, recv2)
+    right_out[...] = right / scale
+
+
+def ar_scratch(width):
+    return [
+        pltpu.VMEM((GROUP, RANK, width), F32),
+        pltpu.VMEM((GROUP, RANK, width), F32),
+        pltpu.VMEM((NZ, RANK, width), F32),
+        pltpu.VMEM((GROUP, RANK, width), F32),
+        pltpu.SemaphoreType.DMA((3, 8)),
+        pltpu.SemaphoreType.DMA((3, 8)),
+    ]
+
+
+def powersgd(acts, vg, err, warm, scale):
+    vmem = pl.BlockSpec(memory_space=pltpu.VMEM)
+    return pl.pallas_call(
+        functools.partial(powersgd_kernel, scale),
+        out_shape=(
+            jax.ShapeDtypeStruct((RANK, acts.shape[1]), F32),
+            jax.ShapeDtypeStruct((RANK, vg.shape[1]), F32),
+        ),
+        in_specs=[vmem] * 4,
+        out_specs=(vmem, vmem),
+        scratch_shapes=ar_scratch(384) + ar_scratch(256),
+        compiler_params=pltpu.CompilerParams(
+            collective_id=1, has_side_effects=True, vmem_limit_bytes=40 << 20),
+    )(acts, vg, err, warm)
+
+
 MICRO = 4
-DP = ("dp_0", "dp_1", "dp_2")
-
-
-HIGHEST_PRECISION = lax.Precision.HIGHEST
+DP = ("y", "z", "core")
 
 
 def in_one_piece(arrays, axis, dim, along):
@@ -27,32 +181,6 @@
     peers = lax.axis_size(axis)
     pairs = [(i, i + by) for i in range(peers) if 0 <= i + by < peers]
     return lax.ppermute(value, axis, pairs)
-
-
-def one_axis_at_a_time(value, axes):
-    return functools.reduce(lax.psum, axes, value)
-
-
-def from_everyone(value, axis):
-    peers = lax.axis_size(axis)
-    return lax.all_to_all(
-        jnp.broadcast_to(value[None], (peers, *value.shape)), axis, 0, 0, tiled=True
-    )
-
-
-def taken_together(value, axis):
-    return from_everyone(value, axis).sum(axis=0)
-
-
-def orthonormal(vectors):
-    result = []
-    for column in range(vectors.shape[0]):
-        current = vectors[column]
-        for previous in result:
-            current = current - jnp.mean(current * previous) * previous
-        current = current / jnp.sqrt(jnp.mean(current * current) + 1e-06)
-        result.append(current)
-    return jnp.stack(result)
 
 
 def local(acts, gates, w_value, w_out, residual_error, grad_top, warm_factor):
@@ -89,31 +217,14 @@
         )
         if step_index + 1 < turn_count:
             incoming = shifted(passed, "section", -1)
-    warm_start = warm_factor[0]
-    grads_wide = value_grads.astype(jnp.float32)
-    inputs_wide = inputs.astype(jnp.float32)
-    error_wide = residual_error[0].astype(jnp.float32)
-    projected = jnp.dot(grads_wide, warm_start.T, precision=HIGHEST_PRECISION)
-    factor = lax.dot_general(
-        projected, inputs_wide, (((0,), (0,)), ((), ())), precision=HIGHEST_PRECISION
-    )
-    factor = factor + lax.dot_general(
-        warm_start, error_wide, (((1,), (1,)), ((), ())), precision=HIGHEST_PRECISION
-    )
-    factor_total = one_axis_at_a_time(factor, DP)
-    basis_rows = orthonormal(factor_total)
-    mapped = jnp.dot(inputs_wide, basis_rows.T, precision=HIGHEST_PRECISION)
-    second = lax.dot_general(
-        mapped, grads_wide, (((0,), (0,)), ((), ())), precision=HIGHEST_PRECISION
-    )
-    second = second + jnp.dot(basis_rows, error_wide, precision=HIGHEST_PRECISION)
-    second = taken_together(second, DP) / math.sqrt(row_count * lax.axis_size(DP) * model_width)
+    scale = math.sqrt(row_count * lax.axis_size(DP) * model_width)
+    basis_rows, second = powersgd(inputs, value_grads, residual_error[0], warm_factor[0], scale)
     return (passed_rows[None], basis_rows[None], second[None])
 
 
 def solution(mesh):
     finer = Mesh(
-        mesh.devices.reshape(mesh.shape["section"], 4, 8, 2), ("section", "dp_0", "dp_1", "dp_2")
+        mesh.devices.reshape(mesh.shape["section"], 4, 8, 2), ("section", "y", "z", "core")
     )
     return jax.shard_map(
         local,

time: 349 us -> 274 us (0.79)
  blocking collectives: 53.8 us -> 0 us
  Pallas kernels: 0 us -> 37.8 us
  waiting for transfers between devices: 165 us -> 142 us
  matrix products: 83.3 us -> 66.5 us
  between operations: 21 us -> 14.3 us
  starting transfers between devices: 14.3 us -> 8.08 us
  other arithmetic: 7.68 us -> 1.64 us
    psum x3 -> x0, blocking collectives: 53.8 us -> none  [one_axis_at_a_time(): return functools.reduce(lax.psum, axes, value)]
    pallas_call x0 -> x1, Pallas kernels: none -> 37.8 us  [powersgd(): pl.pallas_call(functools.partial(powersgd_kernel, scale), out_shape=(jax....]
    all_to_all x1 -> x0, waiting for transfers between devices: 25 us -> none  [from_everyone(): lax.all_to_all(jnp.broadcast_to(value[None], (peers, *value.shape)), axis...]
    dot_general x6 -> x0, matrix products: 12.7 us -> none  [the longest x1 5.15 us: local(): lax.dot_general(warm_start, error_wide, (((1,), (1,)), ((), ())), precisi...]
    all_to_all x1 -> x0, starting transfers between devices: 6.36 us -> none  [from_everyone(): lax.all_to_all(jnp.broadcast_to(value[None], (peers, *value.shape)), axis...]
    reduce_sum x7 -> x0, other arithmetic: 3.88 us -> none  [the longest x4 2.44 us: orthonormal(): current = current - jnp.mean(current * previous) * previous]
    dot_general x7, matrix products: 40.5 us -> 36.8 us  [local(): lax.dot_general(value_grad, value_full, (((1,), (1,)), ((), ())), preferr...]
  transfers between devices with their start and end apart: 8 -> 7, of which waited for: 8 -> 7; matrix products, arithmetic and copies ran while one was open for 4% -> 1% of each run, Pallas kernels for 0% -> 0%
where the time goes in v1:
time: 274 us; the launch traced here: 273 us
  waiting for transfers between devices  142 us (52%)
  matrix products  66.5 us (24%)
  Pallas kernels  37.8 us (14%)
  between operations  14.3 us (5%)
  starting transfers between devices  8.08 us (3%)
  local copies, waits for them, and re-layouts  2.9 us (1%)
    all_gather x1, waiting for transfers between devices, in_one_piece(): lax.all_gather(both, axis, axis=dim, tiled=True)  97.3 us
    ppermute x6, waiting for transfers between devices, shifted(): return lax.ppermute(value, axis, pairs)  45 us
    pallas_call x1, Pallas kernels, powersgd(): pl.pallas_call(functools.partial(powersgd_kernel, scale), out_shape=(jax....  37.8 us
    dot_general x7, matrix products, local(): lax.dot_general(value_grad, value_full, (((1,), (1,)), ((), ())), preferr...  36.8 us
    dot_general x7, matrix products, local(): hidden = jnp.dot(arriving, out_full, preferred_element_type=jnp.float32)  29.7 us
    ppermute x6, starting transfers between devices, shifted(): return lax.ppermute(value, axis, pairs)  8.04 us
  transfers between devices with their start and end apart: 7, of which 7 were waited for; matrix products, arithmetic and copies ran while one was open for 1% of the time, Pallas kernels for 0%

profile of v1, /device:TPU:1, one launch (start us, length us, event | category | flops | bytes accessed | tf_op | source)
XLA Modules:
  0.0 273.4 jit_solution(11546783691232464252)
XLA Ops:
  7.2 0.0 all-gather.2.cloned.1.call-start
  7.2 1.6 pad_maximum_fusion
  8.8 0.0 all-gather.2.cloned.1.call-update
  8.9 97.3 %all-gather.2.cloned.1.call-done = bf16[2560,2560]{1,0:T(8,128)(2,1)} async-done(((bf16[40,2560]{1,0:T(8,128)(2,1)}), bf16[2560,2560]{1,0:T(8,128)(2,1)}) %all-gather.2.cloned.1.call-update) | async-done | bytes 13107216 | tf_op jit(solution)/shard_map/all_gather | solution.py:173
  106.2 4.2 %select_dynamic-update-slice_fusion.12 = (bf16[256,1280]{1,0:T(8,128)(2,1)S(1)}, bf16[64,1280]{1,0:T(8,128)(2,1)S(1)}) fusion(bf16[256,1280]{1,0:T(8,128)(2,1)S(1)} %broadcast_in_dim.24, s32[]{:T(128)S(6)} %select_n.218, pred[]{:T(512)S(6)} %and.22, bf16[1,256,1280]{2,1,0:T(8,128)(2,1)} %param.8, bf16[2560,2560]{1,0:T(8,128)(2,1)} %all-gather.2.cloned.1.call-done, ...), kind=kOutput, calls=%fused_computation.65 | convolution fusion | flops 419921920 | bytes 7374848 | tf_op jit(solution)/shard_map/dot_general | solution.py:206
  110.5 0.0 copy-start.4
  110.5 0.1 broadcast_in_dim.20
  110.6 5.0 %select_dynamic-update-slice_fusion.5 = (bf16[256,2560]{1,0:T(8,128)(2,1)S(1)}, bf16[64,2560]{1,0:T(8,128)(2,1)S(1)}) fusion(bf16[256,2560]{1,0:T(8,128)(2,1)S(1)} %broadcast_in_dim.20, s32[]{:T(128)S(6)} %select_n.218, pred[]{:T(512)S(6)} %and.22, bf16[64,1280]{1,0:T(8,128)(2,1)S(1)} %get-tuple-element.20, ...), kind=kOutput, calls=%fused_computation.56 | convolution fusion | flops 420249600 | bytes 7700486 | tf_op jit(solution)/shard_map/dot_general | solution.py:208
  115.6 1.3 collective-permute-start
  116.9 9.6 %collective-permute-done = bf16[64,2560]{1,0:T(8,128)(2,1)S(1)} collective-permute-done((bf16[64,2560]{1,0:T(8,128)(2,1)S(1)}, bf16[64,2560]{1,0:T(8,128)(2,1)S(1)}, u32[]{:S(2)}, u32[]{:S(2)}) %collective-permute-start) | collective-permute-done | bytes 327712 | tf_op jit(solution)/shard_map/ppermute | solution.py:183
  126.5 0.0 copy-done.4
  126.5 4.2 %select_dynamic-update-slice_fusion.11 = (bf16[256,1280]{1,0:T(8,128)(2,1)S(1)}, bf16[64,1280]{1,0:T(8,128)(2,1)S(1)}) fusion(bf16[256,1280]{1,0:T(8,128)(2,1)S(1)} %get-tuple-element.19, s32[]{:T(128)S(6)} %select_n.223, pred[]{:T(512)S(6)} %and.23, bf16[1,256,1280]{2,1,0:T(8,128)(2,1)S(1)} %copy-done.4, ...), kind=kOutput, calls=%fused_computation.64 | convolution fusion | flops 419921920 | bytes 7866368 | tf_op jit(solution)/shard_map/dot_general | solution.py:206
  130.7 5.0 %select_dynamic-update-slice_fusion.4 = (bf16[256,2560]{1,0:T(8,128)(2,1)S(1)}, bf16[64,2560]{1,0:T(8,128)(2,1)S(1)}) fusion(bf16[256,2560]{1,0:T(8,128)(2,1)S(1)} %get-tuple-element.17, s32[]{:T(128)S(6)} %select_n.223, pred[]{:T(512)S(6)} %and.23, bf16[64,2560]{1,0:T(8,128)(2,1)S(1)} %collective-permute-done, bf16[256,2560]{1,0:T(8,128)(2,1)} %param.12, ...), kind=kOutput, calls=%fused_computation.54 | convolution fusion | flops 420249600 | bytes 8355846 | tf_op jit(solution)/shard_map/dot_general | solution.py:208
  135.7 1.3 collective-permute-start.1
  137.0 8.7 %collective-permute-done.1 = bf16[64,2560]{1,0:T(8,128)(2,1)S(1)} collective-permute-done((bf16[64,2560]{1,0:T(8,128)(2,1)S(1)}, bf16[64,2560]{1,0:T(8,128)(2,1)S(1)}, u32[]{:S(2)}, u32[]{:S(2)}) %collective-permute-start.1) | collective-permute-done | bytes 327712 | tf_op jit(solution)/shard_map/ppermute | solution.py:183
  145.8 4.2 %select_dynamic-update-slice_fusion.10 = (bf16[256,1280]{1,0:T(8,128)(2,1)S(1)}, bf16[64,1280]{1,0:T(8,128)(2,1)S(1)}) fusion(bf16[256,1280]{1,0:T(8,128)(2,1)S(1)} %get-tuple-element.21, s32[]{:T(128)S(6)} %select_n.229, pred[]{:T(512)S(6)} %and.24, bf16[1,256,1280]{2,1,0:T(8,128)(2,1)S(1)} %copy-done.4, ...), kind=kOutput, calls=%fused_computation.63 | convolution fusion | flops 419921920 | bytes 7866368 | tf_op jit(solution)/shard_map/dot_general | solution.py:206
  150.0 5.0 %select_dynamic-update-slice_fusion.3 = (bf16[256,2560]{1,0:T(8,128)(2,1)S(1)}, bf16[64,2560]{1,0:T(8,128)(2,1)S(1)}) fusion(bf16[256,2560]{1,0:T(8,128)(2,1)S(1)} %get-tuple-element.15, s32[]{:T(128)S(6)} %select_n.229, pred[]{:T(512)S(6)} %and.24, bf16[64,2560]{1,0:T(8,128)(2,1)S(1)} %collective-permute-done.1, bf16[256,2560]{1,0:T(8,128)(2,1)} %param.12, ...), kind=kOutput, calls=%fused_computation.52 | convolution fusion | flops 420249600 | bytes 8355846 | tf_op jit(solution)/shard_map/dot_general | solution.py:208
  155.0 1.3 collective-permute-start.2
  156.3 7.9 %collective-permute-done.2 = bf16[64,2560]{1,0:T(8,128)(2,1)S(1)} collective-permute-done((bf16[64,2560]{1,0:T(8,128)(2,1)S(1)}, bf16[64,2560]{1,0:T(8,128)(2,1)S(1)}, u32[]{:S(2)}, u32[]{:S(2)}) %collective-permute-start.2) | collective-permute-done | bytes 327712 | tf_op jit(solution)/shard_map/ppermute | solution.py:183
  164.2 4.2 %select_dynamic-update-slice_fusion.9 = (bf16[256,1280]{1,0:T(8,128)(2,1)S(1)}, bf16[64,1280]{1,0:T(8,128)(2,1)S(1)}) fusion(bf16[256,1280]{1,0:T(8,128)(2,1)S(1)} %get-tuple-element.23, s32[]{:T(128)S(6)} %select_n.235, pred[]{:T(512)S(6)} %and.25, bf16[1,256,1280]{2,1,0:T(8,128)(2,1)S(1)} %copy-done.4, ...), kind=kOutput, calls=%fused_computation.62 | convolution fusion | flops 419921920 | bytes 7866368 | tf_op jit(solution)/shard_map/dot_general | solution.py:206
  168.4 5.0 %select_dynamic-update-slice_fusion.2 = (bf16[256,2560]{1,0:T(8,128)(2,1)S(1)}, bf16[64,2560]{1,0:T(8,128)(2,1)S(1)}) fusion(bf16[256,2560]{1,0:T(8,128)(2,1)S(1)} %get-tuple-element.13, s32[]{:T(128)S(6)} %select_n.235, pred[]{:T(512)S(6)} %and.25, bf16[64,2560]{1,0:T(8,128)(2,1)S(1)} %collective-permute-done.2, bf16[256,2560]{1,0:T(8,128)(2,1)} %param.12, ...), kind=kOutput, calls=%fused_computation.50 | convolution fusion | flops 420249600 | bytes 8355846 | tf_op jit(solution)/shard_map/dot_general | solution.py:208
  173.4 1.3 collective-permute-start.3
  174.7 7.0 %collective-permute-done.3 = bf16[64,2560]{1,0:T(8,128)(2,1)S(1)} collective-permute-done((bf16[64,2560]{1,0:T(8,128)(2,1)S(1)}, bf16[64,2560]{1,0:T(8,128)(2,1)S(1)}, u32[]{:S(2)}, u32[]{:S(2)}) %collective-permute-start.3) | collective-permute-done | bytes 327712 | tf_op jit(solution)/shard_map/ppermute | solution.py:183
  181.7 4.2 %select_dynamic-update-slice_fusion.8 = (bf16[256,1280]{1,0:T(8,128)(2,1)S(1)}, bf16[64,1280]{1,0:T(8,128)(2,1)S(1)}) fusion(bf16[256,1280]{1,0:T(8,128)(2,1)S(1)} %get-tuple-element.25, s32[]{:T(128)S(6)} %select_n.241, pred[]{:T(512)S(6)} %and.26, bf16[1,256,1280]{2,1,0:T(8,128)(2,1)S(1)} %copy-done.4, ...), kind=kOutput, calls=%fused_computation.61 | convolution fusion | flops 419921920 | bytes 7866368 | tf_op jit(solution)/shard_map/dot_general | solution.py:206
  186.0 5.7 %select_dynamic-update-slice_fusion.1 = (bf16[256,2560]{1,0:T(8,128)(2,1)S(1)}, bf16[64,2560]{1,0:T(8,128)(2,1)}) fusion(bf16[256,2560]{1,0:T(8,128)(2,1)S(1)} %get-tuple-element.11, s32[]{:T(128)S(6)} %select_n.241, pred[]{:T(512)S(6)} %and.26, bf16[64,2560]{1,0:T(8,128)(2,1)S(1)} %collective-permute-done.3, bf16[256,2560]{1,0:T(8,128)(2,1)} %param.12, ...), kind=kOutput, calls=%fused_computation.48 | convolution fusion | flops 420249600 | bytes 8355846 | tf_op jit(solution)/shard_map/dot_general | solution.py:208
  191.7 0.0 copy-start.2
  191.7 1.3 collective-permute-start.4
  193.0 6.7 %collective-permute-done.4 = bf16[64,2560]{1,0:T(8,128)(2,1)S(1)} collective-permute-done((bf16[64,2560]{1,0:T(8,128)(2,1)}, bf16[64,2560]{1,0:T(8,128)(2,1)S(1)}, u32[]{:S(2)}, u32[]{:S(2)}) %collective-permute-start.4) | collective-permute-done | bytes 327712 | tf_op jit(solution)/shard_map/ppermute | solution.py:183
  199.7 4.2 %select_dynamic-update-slice_fusion.7 = (bf16[256,1280]{1,0:T(8,128)(2,1)S(1)}, bf16[64,1280]{1,0:T(8,128)(2,1)S(1)}) fusion(bf16[256,1280]{1,0:T(8,128)(2,1)S(1)} %get-tuple-element.27, s32[]{:T(128)S(6)} %select_n.247, pred[]{:T(512)S(6)} %and.27, bf16[1,256,1280]{2,1,0:T(8,128)(2,1)S(1)} %copy-done.4, ...), kind=kOutput, calls=%fused_computation.60 | convolution fusion | flops 419921920 | bytes 7866368 | tf_op jit(solution)/shard_map/dot_general | solution.py:206
  203.9 0.0 copy-done.2
  203.9 0.0 slice-start
  203.9 6.0 %select_dynamic-update-slice_fusion = (bf16[256,2560]{1,0:T(8,128)(2,1)}, bf16[64,2560]{1,0:T(8,128)(2,1)}) fusion(bf16[256,2560]{1,0:T(8,128)(2,1)} %copy-done.2, s32[]{:T(128)S(6)} %select_n.247, pred[]{:T(512)S(6)} %and.27, bf16[64,2560]{1,0:T(8,128)(2,1)S(1)} %collective-permute-done.4, bf16[256,2560]{1,0:T(8,128)(2,1)} %param.12, pred[]{:T(512)S(6)} %eq.2, ...), kind=kOutput, calls=%fused_computation.46 | convolution fusion | flops 420249600 | bytes 8355846 | tf_op jit(solution)/shard_map/dot_general | solution.py:208
  210.0 1.6 collective-permute-start.5
  211.6 0.0 copy-start
  211.6 0.0 slice-start.1
  211.6 1.5 copy.23
  213.1 5.0 %collective-permute-done.5 = bf16[64,2560]{1,0:T(8,128)(2,1)S(1)} collective-permute-done((bf16[64,2560]{1,0:T(8,128)(2,1)}, bf16[64,2560]{1,0:T(8,128)(2,1)S(1)}, u32[]{:S(2)}, u32[]{:S(2)}) %collective-permute-start.5) | collective-permute-done | bytes 327712 | tf_op jit(solution)/shard_map/ppermute | solution.py:183
  218.1 4.2 %select_dynamic-update-slice_fusion.6 = (bf16[256,1280]{1,0:T(8,128)(2,1)S(1)}, bf16[64,1280]{1,0:T(8,128)(2,1)S(1)}) fusion(bf16[256,1280]{1,0:T(8,128)(2,1)S(1)} %get-tuple-element.29, s32[]{:T(128)S(6)} %select_n.253, pred[]{:T(512)S(6)} %and.28, bf16[1,256,1280]{2,1,0:T(8,128)(2,1)} %param.8, bf16[2560,2560]{1,0:T(8,128)(2,1)} %all-gather.2.cloned.1.call-done, ...), kind=kOutput, calls=%fused_computation.59 | convolution fusion | flops 419921920 | bytes 7866368 | tf_op jit(solution)/shard_map/dot_general | solution.py:206
  222.4 0.0 slice-done
  222.4 0.0 copy-done.1
  222.4 0.0 copy-done
  222.4 0.0 slice-done.1
  222.4 37.8 %shard_map.94 = (f32[4,2560]{1,0:T(4,128)S(1)}, f32[4,1280]{1,0:T(4,128)S(1)}) custom-call(bf16[256,2560]{1,0:T(8,128)(2,1)S(1)} %bitcast.43, bf16[256,1280]{1,0:T(8,128)(2,1)S(1)} %get-tuple-element.31.vg, bf16[2560,1280]{1,0:T(8,128)(2,1)S(1)} %bitcast.42, f32[4,1280]{1,0:T(4,128)S(1)} %bitcast.45), custom_call_target="tpu_custom_call" | custom-call | tf_op jit(solution)/shard_map/pallas_call | solution.py:153
  260.2 5.1 %fusion.30 = bf16[1,256,2560]{2,1,0:T(8,128)(2,1)S(1)} fusion(bf16[1,256,2560]{2,1,0:T(8,128)(2,1)S(1)} %copy.23, s32[]{:T(128)S(6)} %select_n.253, bf16[256,2560]{1,0:T(8,128)(2,1)} %get-tuple-element.7, pred[]{:T(512)S(6)} %and.28, bf16[64,2560]{1,0:T(8,128)(2,1)S(1)} %collective-permute-done.5, bf16[256,2560]{1,0:T(8,128)(2,1)} %param.12, pred[]{:T(512)S(6)} %eq.2, ...), kind=kOutput, calls=%fused_computation.44 | convolution fusion | flops 420249600 | bytes 8028166 | tf_op jit(solution)/shard_map/dot_general | solution.py:208
  265.3 0.0 copy-start.3
  265.3 0.7 copy.26
  266.0 0.6 copy.27
  266.6 0.0 copy-done.3
  (3 shorter events, 0.0 us)
Async XLA Ops:
  7.2 99.0 %all-gather.2.cloned.1.call-start = ((), (), s32[]{:S(2)}) async-start(), calls=%async_computation | async-start | bytes 13312000 | tf_op jit(solution)/shard_map/all_gather | solution.py:173
  110.5 16.0 %copy-start.4 = (bf16[1,256,1280]{2,1,0:T(8,128)(2,1)S(1)}, bf16[1,256,1280]{2,1,0:T(8,128)(2,1)}, u32[]{:S(2)}) copy-start(bf16[1,256,1280]{2,1,0:T(8,128)(2,1)} %param.8) | copy-start | bytes 1966084
  115.6 10.9 %collective-permute-start = (bf16[64,2560]{1,0:T(8,128)(2,1)S(1)}, bf16[64,2560]{1,0:T(8,128)(2,1)S(1)}, u32[]{:S(2)}, u32[]{:S(2)}) collective-permute-start(bf16[64,2560]{1,0:T(8,128)(2,1)S(1)} %get-tuple-element.18), channel_id=1, source_target_pairs={{64,0},{128,64},{192,128},{65,1},{129,65},{193,129},{66,2},{130,66... | collective-permute-start | bytes 983048 | tf_op jit(solution)/shard_map/ppermute | solution.py:183
  135.7 10.0 %collective-permute-start.1 = (bf16[64,2560]{1,0:T(8,128)(2,1)S(1)}, bf16[64,2560]{1,0:T(8,128)(2,1)S(1)}, u32[]{:S(2)}, u32[]{:S(2)}) collective-permute-start(bf16[64,2560]{1,0:T(8,128)(2,1)S(1)} %get-tuple-element.16), channel_id=1, source_target_pairs={{64,0},{128,64},{192,128},{65,1},{129,65},{193,129},{66,2},{130,66... | collective-permute-start | bytes 983048 | tf_op jit(solution)/shard_map/ppermute | solution.py:183
  155.0 9.2 %collective-permute-start.2 = (bf16[64,2560]{1,0:T(8,128)(2,1)S(1)}, bf16[64,2560]{1,0:T(8,128)(2,1)S(1)}, u32[]{:S(2)}, u32[]{:S(2)}) collective-permute-start(bf16[64,2560]{1,0:T(8,128)(2,1)S(1)} %get-tuple-element.14), channel_id=1, source_target_pairs={{64,0},{128,64},{192,128},{65,1},{129,65},{193,129},{66,2},{130,66... | collective-permute-start | bytes 983048 | tf_op jit(solution)/shard_map/ppermute | solution.py:183
  173.4 8.3 %collective-permute-start.3 = (bf16[64,2560]{1,0:T(8,128)(2,1)S(1)}, bf16[64,2560]{1,0:T(8,128)(2,1)S(1)}, u32[]{:S(2)}, u32[]{:S(2)}) collective-permute-start(bf16[64,2560]{1,0:T(8,128)(2,1)S(1)} %get-tuple-element.12), channel_id=1, source_target_pairs={{64,0},{128,64},{192,128},{65,1},{129,65},{193,129},{66,2},{130,66... | collective-permute-start | bytes 983048 | tf_op jit(solution)/shard_map/ppermute | solution.py:183
  191.7 12.3 %copy-start.2 = (bf16[256,2560]{1,0:T(8,128)(2,1)}, bf16[256,2560]{1,0:T(8,128)(2,1)S(1)}, u32[]{:S(2)}) copy-start(bf16[256,2560]{1,0:T(8,128)(2,1)S(1)} %get-tuple-element.9) | copy-start | bytes 3932164
  191.7 8.0 %collective-permute-start.4 = (bf16[64,2560]{1,0:T(8,128)(2,1)}, bf16[64,2560]{1,0:T(8,128)(2,1)S(1)}, u32[]{:S(2)}, u32[]{:S(2)}) collective-permute-start(bf16[64,2560]{1,0:T(8,128)(2,1)} %get-tuple-element.10), channel_id=1, source_target_pairs={{64,0},{128,64},{192,128},{65,1},{129,65},{193,129},{66,2},{130,66... | collective-permute-start | bytes 983048 | tf_op jit(solution)/shard_map/ppermute | solution.py:183
  203.9 18.5 %slice-start = ((s8[6553600]{0:T(1024)(128)(4,1)}), s8[2359296]{0:T(1024)(128)(4,1)S(1)}, s32[]{:S(2)}) async-start(s8[6553600]{0:T(1024)(128)(4,1)} %bitcast.40), calls=%async_computation.1 | async-start | bytes 4718592
  210.0 12.4 %copy-start.1 = (f32[1,4,1280]{2,1,0:T(4,128)S(1)}, f32[1,4,1280]{2,1,0:T(4,128)}, u32[]{:S(2)}) copy-start(f32[1,4,1280]{2,1,0:T(4,128)} %param.13) | copy-start | bytes 61444
  210.0 8.1 %collective-permute-start.5 = (bf16[64,2560]{1,0:T(8,128)(2,1)}, bf16[64,2560]{1,0:T(8,128)(2,1)S(1)}, u32[]{:S(2)}, u32[]{:S(2)}) collective-permute-start(bf16[64,2560]{1,0:T(8,128)(2,1)} %get-tuple-element.8), channel_id=1, source_target_pairs={{64,0},{128,64},{192,128},{65,1},{129,65},{193,129},{66,2},{130,66... | collective-permute-start | bytes 983048 | tf_op jit(solution)/shard_map/ppermute | solution.py:183
  211.6 10.8 %copy-start = (bf16[1,256,2560]{2,1,0:T(8,128)(2,1)S(1)}, bf16[1,256,2560]{2,1,0:T(8,128)(2,1)}, u32[]{:S(2)}) copy-start(bf16[1,256,2560]{2,1,0:T(8,128)(2,1)} %param.7) | copy-start | bytes 3932164
  211.6 10.8 %slice-start.1 = ((s8[6553600]{0:T(1024)(128)(4,1)}), s8[4194304]{0:T(1024)(128)(4,1)S(1)}, s32[]{:S(2)}) async-start(s8[6553600]{0:T(1024)(128)(4,1)} %bitcast.40), calls=%async_computation.2 | async-start | bytes 8388608
  265.3 1.3 copy-start.3
Sparse Core Ops, SparseCore 0:
  11.3 94.8 all-gather.1
